TPU v7x, 32 devices: a whole 2x2x4 slice. The times are simulated.
32 devices in a mesh: section: 2 (over x), dp: 16 (over z, y, core).
Axes of the slice: x: 2, y: 2, z: 4, core: 2. Of those that a mesh axis runs over, the one named last changes fastest.
Arguments:
- grads: bfloat16 [32, 524288], P(('section', 'dp')), parts along dimension 0, may hold values from -6 to 6
- master: float32 [32, 32768], P(('section', 'dp')), parts along dimension 0, may hold values from -30 to 30
- first_moment: float32 [32, 32768], P(('section', 'dp')), parts along dimension 0, may hold values from -0.6 to 0.6
- second_moment: float32 [32, 32768], P(('section', 'dp')), parts along dimension 0, may hold values from 0.005 to 0.05
- perm: int32 [32], P('section'), parts along dimension 0, may hold values from 0 to 15, each once
- bounds: int32 [34], P('section'), parts along dimension 0, may hold values from 0 to 524288, as said below
Outputs:
- new_weights: bfloat16 [1048576], P('section'), parts along dimension 0
- new_master: float32 [32, 32768], P(('section', 'dp')), parts along dimension 0
- new_first: float32 [32, 32768], P(('section', 'dp')), parts along dimension 0
- new_second: float32 [32, 32768], P(('section', 'dp')), parts along dimension 0
- step_taken: float32 [32, 32768], P(('section', 'dp')), parts along dimension 0
There are 2 independent parts, one for each index of `section`. A program takes and returns all parts, laid end to end along the dimension named above; each array names one. Nothing has to cross between parts.
Inputs may be any that keep to these rules, and one draw needn't show every extreme that they name: `perm`: each device index appears exactly once. `bounds`: strictly increasing multiples of 128, the first 0 and the last 524288.
All inputs are finite; a program needn't handle non-finite values.
Results may differ from a plain program's by a relative error of at most 0.0004.
Values may be sent and summed in bfloat16 or wider, within the bound.
A program may use at most 128 MiB of HBM per device.

v0:
```python
import jax
import jax.numpy as jnp
from jax import lax
from jax.sharding import PartitionSpec as P

beta_first = 0.9
beta_second = 0.999
first_fix = 1.0 - 0.9**10
second_fix = 1.0 - 0.999**10
adam_eps = 1e-06
norm_eps = 1e-06
decay_rate = 0.01
learn_rate = 0.01


def per_device(grads, master, first_moment, second_moment, perm, bounds):
    replica_count = lax.axis_size("dp")
    shard_len = master.shape[1]
    own_block = perm[lax.axis_index("dp")]
    positions = own_block * shard_len + jnp.arange(shard_len, dtype=jnp.int32)
    member = (positions[None, :] >= bounds[:-1, None]) & (positions[None, :] < bounds[1:, None])
    onehot = member.astype(jnp.float32)
    weight_part = jnp.dot(onehot, master[0] * master[0], precision=lax.Precision.HIGHEST)
    summed = lax.psum(grads[0].astype(jnp.float32), "dp")
    own_grad = (
        lax.dynamic_slice_in_dim(summed, own_block * shard_len, shard_len)[None, :] / replica_count
    )
    new_first = beta_first * first_moment + (1.0 - beta_first) * own_grad
    new_second = beta_second * second_moment + (1.0 - beta_second) * own_grad * own_grad
    direction = (
        new_first / first_fix / (jnp.sqrt(new_second / second_fix) + adam_eps) + decay_rate * master
    )
    update_part = jnp.dot(onehot, direction[0] * direction[0], precision=lax.Precision.HIGHEST)
    weight_sq, update_sq = lax.psum((weight_part, update_part), "dp")
    trust_ratio = jnp.sqrt(weight_sq) / (jnp.sqrt(update_sq) + norm_eps)
    entry_ratio = jnp.dot(trust_ratio, onehot, precision=lax.Precision.HIGHEST)
    step_taken = entry_ratio[None, :] * direction
    new_master = master - learn_rate * step_taken
    gathered = lax.all_gather(new_master.astype(jnp.bfloat16), "dp", axis=0, tiled=True)
    inverse = jnp.argsort(perm)
    new_weights = jnp.take(gathered, inverse, axis=0).reshape(-1)
    return (new_weights, new_master, new_first, new_second, step_taken)


def solution(mesh):
    return jax.shard_map(
        per_device,
        mesh=mesh,
        in_specs=(
            P(("section", "dp"), None),
            P(("section", "dp"), None),
            P(("section", "dp"), None),
            P(("section", "dp"), None),
            P("section"),
            P("section"),
        ),
        out_specs=(
            P("section"),
            P(("section", "dp"), None),
            P(("section", "dp"), None),
            P(("section", "dp"), None),
            P(("section", "dp"), None),
        ),
        check_vma=False,
    )
```

profile of v0, /device:TPU:9, one launch (start us, length us, event | category | flops | bytes accessed | tf_op | source)
XLA Modules:
  0.0 198.1 jit_solution(13734129077697938728)
XLA Ops:
  7.2 0.0 all-reduce.3.cloned.1.call-start
  7.2 4.8 %convert_element_type.13 = f32[1,524288]{1,0:T(1,128)} convert(bf16[1,524288]{1,0:T(2,128)(2,1)} %param.6) | non-fusion elementwise | flops 524288 | bytes 3145728 | tf_op jit(solution)/shard_map/convert_element_type | solution.py:24
  12.0 0.0 copy-start.5
  12.0 0.0 copy-start
  12.0 0.0 copy-start.2
  12.0 0.0 copy-start.3
  12.0 0.0 all-reduce.3.cloned.1.call-update
  12.0 0.0 all-gather.3.cloned.1.call-start
  12.1 0.6 copy-done.5
  12.7 0.6 dynamic_slice.6
  13.9 0.0 copy-done.4
  13.9 0.1 fusion.17
  14.0 0.0 copy-done
  14.0 1.6 fusion.2
  15.6 94.8 %all-reduce.3.cloned.1.call-done = f32[524288]{0:T(1024)} async-done(((f32[524288]{0:T(1024)}), f32[524288]{0:T(1024)}) %all-reduce.3.cloned.1.call-update) | async-done | bytes 2097168 | tf_op jit(solution)/shard_map/psum | solution.py:24
  110.4 0.9 multiply_multiply_fusion
  111.4 0.0 copy-done.2
  111.4 0.0 copy-done.3
  111.4 1.4 multiply_add_fusion
  112.8 1.6 fusion.3
  114.4 23.9 %all-reduce = (f32[16]{0:T(128)S(1)}, f32[16]{0:T(128)S(1)}) all-reduce(f32[16]{0:T(128)S(1)} %fusion.3, f32[16]{0:T(128)S(1)} %fusion.2), channel_id=1, replica_groups=mesh['section'=2,'dp'=16] {'dp'}, use_global_device_ids=true, to_apply=%region_3.0 | all-reduce | flops 32 | bytes 256 | tf_op jit(solution)/shard_map/psum | solution.py:34
  138.3 0.9 convolution_multiply_fusion
  139.2 0.0 copy-start.1
  139.2 0.9 convert_bitcast_fusion
  140.1 0.0 all-gather.3.cloned.1.call-update
  140.2 1.3 sort.17
  141.5 44.4 %all-gather.3.cloned.1.call-done = bf16[16,1,32768]{2,1,0:T(2,128)(2,1)} async-done(((bf16[1,1,32768]{2,1,0:T(2,128)(2,1)}), bf16[16,1,32768]{2,1,0:T(2,128)(2,1)}) %all-gather.3.cloned.1.call-update) | async-done | bytes 1048592 | tf_op jit(solution)/shard_map/all_gather | solution.py:39
  185.9 2.7 %copy.14 = bf16[16,1,32768]{2,0,1:T(8,128)(2,1)S(1)} copy(bf16[16,1,32768]{2,1,0:T(2,128)(2,1)} %all-gather.3.cloned.1.call-done) | data formatting | bytes 2097152
  188.7 1.2 gather_fusion
  189.9 0.0 copy-done.1
  189.9 0.2 select_bitcast_fusion
  190.1 1.2 copy.12
  (6 shorter events, 0.0 us)
Async XLA Ops:
  7.2 103.3 %all-reduce.3.cloned.1.call-start = ((), (), s32[]{:S(2)}) async-start(), calls=%async_computation | async-start | bytes 4194304 | tf_op jit(solution)/shard_map/psum | solution.py:24
  12.0 0.7 copy-start.5
  12.0 1.9 copy-start.4
  12.0 2.0 %copy-start = (f32[1,32768]{1,0:T(1,128)S(1)}, f32[1,32768]{1,0:T(1,128)}, u32[]{:S(2)}) copy-start(f32[1,32768]{1,0:T(1,128)} %param.7) | copy-start | bytes 393220
  12.0 99.3 %copy-start.2 = (f32[1,32768]{1,0:T(1,128)S(1)}, f32[1,32768]{1,0:T(1,128)}, u32[]{:S(2)}) copy-start(f32[1,32768]{1,0:T(1,128)} %param.8) | copy-start | bytes 393220
  12.0 99.4 %copy-start.3 = (f32[1,32768]{1,0:T(1,128)S(1)}, f32[1,32768]{1,0:T(1,128)}, u32[]{:S(2)}) copy-start(f32[1,32768]{1,0:T(1,128)} %param.9) | copy-start | bytes 393220
  12.0 173.9 %all-gather.3.cloned.1.call-start = ((), (), s32[]{:S(2)}) async-start(), calls=%async_computation.1 | async-start | bytes 2228224 | tf_op jit(solution)/shard_map/all_gather | solution.py:39
  139.2 50.7 %copy-start.1 = (f32[1,32768]{1,0:T(1,128)}, f32[1,32768]{1,0:T(1,128)S(1)}, u32[]{:S(2)}) copy-start(f32[1,32768]{1,0:T(1,128)S(1)} %convolution_multiply_fusion) | copy-start | bytes 393220
Sparse Core Ops, SparseCore 0:
  12.2 98.2 all-reduce.2
  140.3 45.5 all-gather.2
where the time goes:
time: 201 us; the launch traced here: 198 us
  waiting for transfers between devices  139 us (69%)
  blocking collectives  23.9 us (12%)
  between operations  14.8 us (7%)
  other arithmetic  9.55 us (5%)
  local copies, waits for them, and re-layouts  6.38 us (3%)
  matrix products  4.16 us (2%)
    psum x1, waiting for transfers between devices, per_device(): summed = lax.psum(grads[0].astype(jnp.float32), 'dp')  94.8 us
    all_gather x1, waiting for transfers between devices, per_device(): lax.all_gather(new_master.astype(jnp.bfloat16), 'dp', axis=0, tiled=True)  44.4 us
    psum x1, blocking collectives, per_device(): weight_sq, update_sq = lax.psum((weight_part, update_part), 'dp')  23.9 us
    convert_element_type x1, other arithmetic, per_device(): summed = lax.psum(grads[0].astype(jnp.float32), 'dp')  4.79 us
    unnamed x14, local copies, waits for them, and re-layouts  4.48 us
  transfers between devices with their start and end apart: 2, of which 2 were waited for; matrix products, arithmetic and copies ran while one was open for 2% of the time, Pallas kernels for 0%

commit v1 on v0

v1 whole, which is shorter than its diff:
```python
import functools

import jax
import jax.numpy as jnp
from jax import lax
from jax.experimental import pallas as pl
from jax.experimental.pallas import tpu as pltpu
from jax.sharding import PartitionSpec as P

beta_first = 0.9
beta_second = 0.999
first_fix = 1.0 - 0.9**10
second_fix = 1.0 - 0.999**10
adam_eps = 1e-06
norm_eps = 1e-06
decay_rate = 0.01
learn_rate = 0.01

LANES = 128
MESH = pl.DeviceIdType.MESH


def member_of(position, ranges):
    return (position >= ranges[0:1, :]) & (position < ranges[8:9, :])


def tensor_sums(member, entries):
    squares = jnp.sum(entries * entries, axis=1, keepdims=True)
    return jnp.sum(jnp.where(member, squares, 0.0), axis=0, keepdims=True)


def arrange(
    n,
    tensors,
    perm_ref,
    bounds_ref,
    grads_ref,
    master_ref,
    first_ref,
    second_ref,
    blocks_out,
    state_out,
    owner_out,
    ranges_out,
    raw,
    sems,
):
    rows = master_ref.shape[0]
    span = rows * LANES
    loads = []
    for d in range(n):
        start = pl.multiple_of(perm_ref[d] * span, LANES)
        source = grads_ref.at[:, pl.ds(start, span)]
        loads.append(pltpu.make_async_copy(source, raw.at[d], sems.at[d]))
    for i, ref in enumerate((master_ref, first_ref, second_ref)):
        loads.append(pltpu.make_async_copy(ref, state_out.at[i], sems.at[n + i]))
    for load in loads:
        load.start()
    lane = lax.broadcasted_iota(jnp.int32, (8, LANES), 1)
    low = jnp.full((8, LANES), 2**30, jnp.int32)
    high = low
    for t in range(tensors):
        here = lax.rem(lane, LANES // 2) == t
        low = jnp.where(here, bounds_ref[t], low)
        high = jnp.where(here, bounds_ref[t + 1], high)
    ranges_out[0:8, :] = low
    ranges_out[8:16, :] = high
    owner_out[...] = perm_ref[lax.axis_index("dp")] * span + LANES * (
        lax.broadcasted_iota(jnp.int32, (rows, LANES), 0)
    )
    for d in range(n):
        loads[d].wait()
        wide = raw[d].astype(jnp.float32).reshape(rows, LANES)
        blocks_out[d] = wide.astype(jnp.bfloat16)
    for load in loads[n:]:
        load.wait()


def kernel(
    n,
    blocks_ref,
    state,
    owner,
    ranges,
    gathered,
    master_out,
    first_out,
    second_out,
    step_out,
    side_recv,
    pair_send,
    pair_recv,
    keep,
    far_send,
    far_recv,
    stats,
    side_sems,
    pair_sems,
    far_sems,
    stat_send_sem,
    stat_recv_sem,
    ag_far_sems,
    ag_side_sems,
    ag_pair_sems,
):
    units = n // 4
    section = lax.axis_index("section")
    me = lax.axis_index("dp")
    core = lax.rem(me, 2)
    side = lax.rem(me // 2, 2)
    rank = me // 4

    def at(index):
        return (section, index)

    def device_of(r, s, c):
        return r * 4 + s * 2 + c

    pair_id = device_of(rank, side, 1 - core)
    side_id = device_of(rank, 1 - side, core)

    barrier = pltpu.get_barrier_semaphore()

    def greet(j, carry):
        pl.semaphore_signal(
            barrier, inc=1, device_id=at(lax.rem(me + j, n)), device_id_type=MESH
        )
        return carry

    lax.fori_loop(1, n, greet, 0)

    sign = jnp.where(2 * rank < units, units - 1, 1)
    order = [lax.rem(rank + sign * (1 + s), units) for s in range(units)]

    def block_of(d):
        return blocks_ref[d].astype(jnp.float32)

    pl.semaphore_wait(barrier, n - 1)
    side_copies = []
    for s in range(units):
        copy = pltpu.make_async_remote_copy(
            src_ref=blocks_ref.at[pl.ds(device_of(order[s], 1 - side, 0), 2)],
            dst_ref=side_recv.at[s],
            send_sem=side_sems.at[0, s],
            recv_sem=side_sems.at[1, s],
            device_id=at(side_id),
            device_id_type=MESH,
        )
        copy.start()
        side_copies.append(copy)

    half = LANES // 2
    low_half = lax.broadcasted_iota(jnp.int32, (1, LANES), 1) < half
    member = member_of(owner[...], ranges)
    weight_row = tensor_sums(member, state[0])

    pair_copies = []
    far_copies = []
    own_sum = None

    def finish(s):
        pair_copies[s].wait_recv()
        total = keep[s] + pair_recv[s]
        if s == units - 1:
            return total
        far_send[s] = total
        copy = pltpu.make_async_remote_copy(
            src_ref=far_send.at[s],
            dst_ref=far_recv.at[rank],
            send_sem=far_sems.at[0, s],
            recv_sem=far_sems.at[1, rank],
            device_id=at(device_of(order[s], side, core)),
            device_id_type=MESH,
        )
        copy.start()
        far_copies.append(copy)
        return None

    for s in range(units):
        side_copies[s].wait_recv()
        theirs = device_of(order[s], side, 1 - core)
        mine = device_of(order[s], side, core)
        pair_send[s] = block_of(theirs) + side_recv[s, 1 - core].astype(jnp.float32)
        copy = pltpu.make_async_remote_copy(
            src_ref=pair_send.at[s],
            dst_ref=pair_recv.at[s],
            send_sem=pair_sems.at[0, s],
            recv_sem=pair_sems.at[1, s],
            device_id=at(pair_id),
            device_id_type=MESH,
        )
        copy.start()
        pair_copies.append(copy)
        keep[s] = block_of(mine) + side_recv[s, core].astype(jnp.float32)
        if s >= 1:
            finish(s - 1)
    own_sum = finish(units - 1)

    for j in range(1, units):
        source = lax.rem(rank + j, units)
        pltpu.make_async_remote_copy(
            src_ref=far_send.at[0],
            dst_ref=far_recv.at[source],
            send_sem=far_sems.at[0, 0],
            recv_sem=far_sems.at[1, source],
            device_id=at(side_id),
            device_id_type=MESH,
        ).wait_recv()
        own_sum = own_sum + far_recv[source]

    own_grad = own_sum / n
    new_first = beta_first * state[1] + (1.0 - beta_first) * own_grad
    new_second = beta_second * state[2] + (1.0 - beta_second) * own_grad * own_grad
    direction = (
        new_first / first_fix / (jnp.sqrt(new_second / second_fix) + adam_eps)
        + decay_rate * state[0]
    )
    update_row = tensor_sums(member, direction)
    stat = jnp.where(low_half, weight_row, update_row)
    stats[me] = jnp.broadcast_to(stat, (8, LANES))

    def stat_copy(source, target):
        return pltpu.make_async_remote_copy(
            src_ref=stats.at[source, pl.ds(0, 1)],
            dst_ref=stats.at[source, pl.ds(0, 1)],
            send_sem=stat_send_sem.at[target],
            recv_sem=stat_recv_sem.at[source],
            device_id=at(target),
            device_id_type=MESH,
        )

    def tell(j, carry):
        stat_copy(me, lax.rem(me + j, n)).start()
        return carry

    lax.fori_loop(1, n, tell, 0)
    first_out[...] = new_first
    second_out[...] = new_second

    def hear(j, total):
        other = lax.rem(me + j, n)
        stat_copy(other, other).wait_recv()
        return total + stats[other, pl.ds(0, 1)]

    total = lax.fori_loop(1, n, hear, stat)
    trust_ratio = jnp.sqrt(total) / (
        jnp.sqrt(pltpu.roll(total, half, 1)) + norm_eps
    )
    entry_ratio = jnp.sum(
        jnp.where(member & low_half, trust_ratio, 0.0), axis=1, keepdims=True
    )
    step_taken = entry_ratio * direction
    new_master = state[0] - learn_rate * step_taken
    gathered[me] = new_master.astype(jnp.bfloat16)

    def gather_copy(block, sems, slot, target):
        return pltpu.make_async_remote_copy(
            src_ref=gathered.at[block],
            dst_ref=gathered.at[block],
            send_sem=sems.at[0, slot],
            recv_sem=sems.at[1, slot],
            device_id=at(target),
            device_id_type=MESH,
        )

    waits = []
    ag_side = gather_copy(me, ag_side_sems, rank, side_id)
    ag_side.start()
    waits.append(ag_side)
    for s in range(units - 1):
        copy = pltpu.make_async_remote_copy(
            src_ref=gathered.at[me],
            dst_ref=gathered.at[me],
            send_sem=ag_far_sems.at[0, s],
            recv_sem=ag_far_sems.at[1, rank],
            device_id=at(device_of(order[s], side, core)),
            device_id_type=MESH,
        )
        copy.start()
        waits.append(copy)
    ag_pair = gather_copy(me, ag_pair_sems, 2 * rank + side, pair_id)
    ag_pair.start()
    waits.append(ag_pair)
    master_out[...] = new_master
    step_out[...] = step_taken

    for s in reversed(range(units - 1)):
        source = order[s]
        block = device_of(source, side, core)
        gather_copy(block, ag_far_sems, source, side_id).wait_recv()
        copy = gather_copy(block, ag_side_sems, source, side_id)
        copy.start()
        waits.append(copy)
        copy = gather_copy(block, ag_pair_sems, 2 * source + side, pair_id)
        copy.start()
        waits.append(copy)
    for s in reversed(range(units)):
        source = order[s]
        block = device_of(source, 1 - side, core)
        gather_copy(block, ag_side_sems, source, side_id).wait_recv()
        copy = gather_copy(block, ag_pair_sems, 2 * source + 1 - side, pair_id)
        copy.start()
        waits.append(copy)
    for s in reversed(range(units)):
        for y in range(2):
            block = device_of(order[s], y, 1 - core)
            gather_copy(block, ag_pair_sems, 2 * order[s] + y, pair_id).wait_recv()

    for copy in side_copies + pair_copies + far_copies + waits:
        copy.wait_send()

    def told(j, carry):
        target = lax.rem(me + j, n)
        stat_copy(me, target).wait_send()
        return carry

    lax.fori_loop(1, n, told, 0)

def place(n, perm_ref, gathered, *refs):
    held, (weights_out, *outs, sems) = refs[:4], refs[4:]
    rows = gathered.shape[1]
    copies = []
    for d in range(n):
        start = pl.multiple_of(perm_ref[d] * rows, rows)
        target = weights_out.at[pl.ds(start, rows)]
        copies.append(pltpu.make_async_copy(gathered.at[d], target, sems.at[d]))
    for i, (ref, out) in enumerate(zip(held, outs)):
        copies.append(pltpu.make_async_copy(ref, out, sems.at[n + i]))
    for copy in copies:
        copy.start()
    for copy in copies:
        copy.wait()


def solution(mesh):
    n = mesh.shape["dp"]
    units = n // 4

    def per_device(grads, master, first_moment, second_moment, perm, bounds):
        shard = master.shape[1]
        rows = shard // LANES
        tensors = bounds.shape[0] - 1
        block = (rows, LANES)
        f32 = jnp.float32
        hbm_spec = pl.BlockSpec(memory_space=pltpu.HBM)
        vmem_spec = pl.BlockSpec(memory_space=pltpu.VMEM)
        smem_spec = pl.BlockSpec(memory_space=pltpu.SMEM)
        arranged = pl.pallas_call(
            functools.partial(arrange, n, tensors),
            out_shape=[
                jax.ShapeDtypeStruct((n,) + block, jnp.bfloat16),
                jax.ShapeDtypeStruct((3,) + block, f32),
                jax.ShapeDtypeStruct(block, jnp.int32),
                jax.ShapeDtypeStruct((16, LANES), jnp.int32),
            ],
            in_specs=[smem_spec] * 2 + [hbm_spec] * 4,
            out_specs=[vmem_spec] * 4,
            scratch_shapes=[
                pltpu.VMEM((n, 1, shard), jnp.bfloat16),
                pltpu.SemaphoreType.DMA((n + 3,)),
            ],
            compiler_params=pltpu.CompilerParams(vmem_limit_bytes=32 * 1024 * 1024),
        )(
            perm,
            bounds,
            grads,
            master.reshape(block),
            first_moment.reshape(block),
            second_moment.reshape(block),
        )
        outs = pl.pallas_call(
            functools.partial(kernel, n),
            out_shape=[jax.ShapeDtypeStruct((n,) + block, jnp.bfloat16)]
            + [jax.ShapeDtypeStruct(block, f32)] * 4,
            in_specs=[vmem_spec] * 4,
            out_specs=[vmem_spec] * 5,
            scratch_shapes=[
                pltpu.VMEM((units, 2) + block, jnp.bfloat16),
                pltpu.VMEM((units,) + block, f32),
                pltpu.VMEM((units,) + block, f32),
                pltpu.VMEM((units,) + block, f32),
                pltpu.VMEM((units,) + block, f32),
                pltpu.VMEM((units,) + block, f32),
                pltpu.VMEM((n, 8, LANES), f32),
                pltpu.SemaphoreType.DMA((2, units)),
                pltpu.SemaphoreType.DMA((2, units)),
                pltpu.SemaphoreType.DMA((2, units)),
                pltpu.SemaphoreType.DMA((n,)),
                pltpu.SemaphoreType.DMA((n,)),
                pltpu.SemaphoreType.DMA((2, units)),
                pltpu.SemaphoreType.DMA((2, units)),
                pltpu.SemaphoreType.DMA((2, 2 * units)),
            ],
            compiler_params=pltpu.CompilerParams(
                collective_id=0,
                has_side_effects=True,
                vmem_limit_bytes=32 * 1024 * 1024,
            ),
        )(*arranged)
        outs = pl.pallas_call(
            functools.partial(place, n),
            out_shape=[jax.ShapeDtypeStruct((n * rows, LANES), jnp.bfloat16)]
            + [jax.ShapeDtypeStruct(block, f32)] * 4,
            in_specs=[smem_spec] + [vmem_spec] * 5,
            out_specs=[hbm_spec] * 5,
            scratch_shapes=[pltpu.SemaphoreType.DMA((n + 4,))],
            compiler_params=pltpu.CompilerParams(vmem_limit_bytes=32 * 1024 * 1024),
        )(perm, *outs)
        weights = outs[0].reshape(-1)
        return (weights,) + tuple(out.reshape(1, shard) for out in outs[1:])

    return jax.shard_map(
        per_device,
        mesh=mesh,
        in_specs=(
            P(("section", "dp"), None),
            P(("section", "dp"), None),
            P(("section", "dp"), None),
            P(("section", "dp"), None),
            P("section"),
            P("section"),
        ),
        out_specs=(
            P("section"),
            P(("section", "dp"), None),
            P(("section", "dp"), None),
            P(("section", "dp"), None),
            P(("section", "dp"), None),
        ),
        check_vma=False,
    )
```

time: 201 us -> 56.2 us (0.28); the launches traced: 198 us -> 55.5 us
  waiting for transfers between devices: 139 us -> 0 us
  Pallas kernels: 0 us -> 49.2 us
  blocking collectives: 23.9 us -> 0 us
  between operations: 14.8 us -> 0.66 us
  other arithmetic: 9.55 us -> 0 us
  matrix products: 4.16 us -> 0 us
    psum x1 -> x0, waiting for transfers between devices: 94.8 us -> none  [per_device(): summed = lax.psum(grads[0].astype(jnp.float32), 'dp')]
    pallas_call x0 -> x3, Pallas kernels: none -> 49.2 us  [the longest x1 42.9 us: per_device(): pl.pallas_call(functools.partial(kernel, n), out_shape=[jax.ShapeDtypeStr...]
    all_gather x1 -> x0, waiting for transfers between devices: 44.4 us -> none  [per_device(): lax.all_gather(new_master.astype(jnp.bfloat16), 'dp', axis=0, tiled=True)]
    psum x1 -> x0, blocking collectives: 23.9 us -> none  [per_device(): weight_sq, update_sq = lax.psum((weight_part, update_part), 'dp')]
    convert_element_type x1 -> x0, other arithmetic: 4.79 us -> none  [per_device(): summed = lax.psum(grads[0].astype(jnp.float32), 'dp')]
    dot_general x3 -> x0, matrix products: 4.16 us -> none  [the longest x1 1.62 us: per_device(): jnp.dot(onehot, master[0] * master[0], precision=lax.Precision.HIGHEST)]
    unnamed x14 -> x12, local copies, waits for them, and re-layouts: 4.48 us -> 5.6 us
  transfers between devices with their start and end apart: 2 -> 0, of which waited for: 2 -> 0; matrix products, arithmetic and copies ran while one was open for 2% -> 0% of each run, Pallas kernels for 0% -> 0%
where the time goes in v1:
time: 56.2 us; the launch traced here: 55.5 us
  Pallas kernels  49.2 us (88%)
  local copies, waits for them, and re-layouts  5.6 us (10%)
  between operations  0.66 us (1%)
    pallas_call x1, Pallas kernels, per_device(): pl.pallas_call(functools.partial(kernel, n), out_shape=[jax.ShapeDtypeStr...  42.9 us
    unnamed x12, local copies, waits for them, and re-layouts  5.6 us
    pallas_call x1, Pallas kernels, per_device(): pl.pallas_call(functools.partial(arrange, n, tensors), out_shape=[jax.Sha...  4.52 us
    pallas_call x1, Pallas kernels, per_device(): pl.pallas_call(functools.partial(place, n), out_shape=[jax.ShapeDtypeStru...  1.85 us

profile of v1, /device:TPU:9, one launch (start us, length us, event | category | flops | bytes accessed | tf_op | source)
XLA Modules:
  0.0 55.5 jit_solution(345942428095293265)
XLA Ops:
  0.6 0.0 copy-start
  0.6 1.6 %copy-done = bf16[1,524288]{1,0:T(2,128)(2,1)S(1)} copy-done((bf16[1,524288]{1,0:T(2,128)(2,1)S(1)}, bf16[1,524288]{1,0:T(2,128)(2,1)}, u32[]{:S(2)}) %copy-start) | copy-done | bytes 1048600
  2.2 0.0 copy-start.1
  2.2 0.9 %copy-done.1 = f32[1,32768]{1,0:T(1,128)S(1)} copy-done((f32[1,32768]{1,0:T(1,128)S(1)}, f32[1,32768]{1,0:T(1,128)}, u32[]{:S(2)}) %copy-start.1) | copy-done | bytes 131096
  3.1 0.0 copy-start.2
  3.1 0.9 %copy-done.2 = f32[1,32768]{1,0:T(1,128)S(1)} copy-done((f32[1,32768]{1,0:T(1,128)S(1)}, f32[1,32768]{1,0:T(1,128)}, u32[]{:S(2)}) %copy-start.2) | copy-done | bytes 131096
  4.0 0.0 copy-start.3
  4.0 0.9 %copy-done.3 = f32[1,32768]{1,0:T(1,128)S(1)} copy-done((f32[1,32768]{1,0:T(1,128)S(1)}, f32[1,32768]{1,0:T(1,128)}, u32[]{:S(2)}) %copy-start.3) | copy-done | bytes 131096
  4.9 0.0 copy-start.4
  4.9 0.7 %copy-done.4 = s32[16]{0:T(128)S(1)} copy-done((s32[16]{0:T(128)S(1)}, s32[16]{0:T(128)}, u32[]{:S(2)}) %copy-start.4) | copy-done | bytes 88
  5.6 0.0 copy-start.5
  5.6 0.7 %copy-done.5 = s32[17]{0:T(128)S(1)} copy-done((s32[17]{0:T(128)S(1)}, s32[17]{0:T(128)}, u32[]{:S(2)}) %copy-start.5) | copy-done | bytes 92
  6.3 4.5 %shard_map.101 = (bf16[16,256,128]{2,1,0:T(8,128)(2,1)S(1)}, f32[3,256,128]{2,1,0:T(8,128)S(1)}, s32[256,128]{1,0:T(8,128)S(1)}, s32[16,128]{1,0:T(8,128)S(1)}) custom-call(s32[16]{0:T(128)S(1)} %copy-done.4, s32[17]{0:T(128)S(1)} %copy-done.5, bf16[1,524288]{1,0:T(2,128)(2,1)S(1)} %copy-done, f32[256,128]{1,0:T(8,128)S(1)} %bitcast.8, ...), custom_call_target="tpu_custom_call" | custom-call | tf_op jit(solution)/shard_map/pallas_call | solution.py:348
  10.8 42.9 %shard_map.102 = (bf16[16,256,128]{2,1,0:T(8,128)(2,1)S(1)}, f32[256,128]{1,0:T(8,128)S(1)}, f32[256,128]{1,0:T(8,128)S(1)}, f32[256,128]{1,0:T(8,128)S(1)}, f32[256,128]{1,0:T(8,128)S(1)}) custom-call(bf16[16,256,128]{2,1,0:T(8,128)(2,1)S(1)} %get-tuple-element.19.blocks_ref, f32[3,256,128]{2,1,0:T(8,128)S(1)} %get-tuple-element.20.state, ...), custom_call_target="tpu_custom_call" | custom-call | tf_op jit(solution)/shard_map/pallas_call | solution.py:371
  53.6 1.8 %shard_map.103 = (bf16[4096,128]{1,0:T(8,128)(2,1)}, f32[256,128]{1,0:T(8,128)}, f32[256,128]{1,0:T(8,128)}, f32[256,128]{1,0:T(8,128)}, f32[256,128]{1,0:T(8,128)}) custom-call(s32[16]{0:T(128)S(1)} %copy-done.4, bf16[16,256,128]{2,1,0:T(8,128)(2,1)S(1)} %get-tuple-element.23.gathered, f32[256,128]{1,0:T(8,128)S(1)} %get-tuple-element.24.refs_0_, ...), custom_call_target="tpu_custom_call" | custom-call | tf_op jit(solution)/shard_map/pallas_call | solution.py:400
Async XLA Ops:
  0.6 1.6 %copy-start = (bf16[1,524288]{1,0:T(2,128)(2,1)S(1)}, bf16[1,524288]{1,0:T(2,128)(2,1)}, u32[]{:S(2)}) copy-start(bf16[1,524288]{1,0:T(2,128)(2,1)} %grads_ref.1) | copy-start | bytes 3145732
  2.2 0.9 %copy-start.1 = (f32[1,32768]{1,0:T(1,128)S(1)}, f32[1,32768]{1,0:T(1,128)}, u32[]{:S(2)}) copy-start(f32[1,32768]{1,0:T(1,128)} %param.7) | copy-start | bytes 393220
  3.1 0.9 %copy-start.2 = (f32[1,32768]{1,0:T(1,128)S(1)}, f32[1,32768]{1,0:T(1,128)}, u32[]{:S(2)}) copy-start(f32[1,32768]{1,0:T(1,128)} %param.8) | copy-start | bytes 393220
  4.0 0.9 %copy-start.3 = (f32[1,32768]{1,0:T(1,128)S(1)}, f32[1,32768]{1,0:T(1,128)}, u32[]{:S(2)}) copy-start(f32[1,32768]{1,0:T(1,128)} %param.9) | copy-start | bytes 393220
  4.9 0.7 %copy-start.4 = (s32[16]{0:T(128)S(1)}, s32[16]{0:T(128)}, u32[]{:S(2)}) copy-start(s32[16]{0:T(128)} %perm_ref.3) | copy-start | bytes 196
  5.6 0.7 %copy-start.5 = (s32[17]{0:T(128)S(1)}, s32[17]{0:T(128)}, u32[]{:S(2)}) copy-start(s32[17]{0:T(128)} %bounds_ref.1) | copy-start | bytes 208

commit v2 on v1

--- a/solution.py
+++ b/solution.py
@@ -17,11 +17,8 @@
 learn_rate = 0.01
 
 LANES = 128
+VMEM_BYTES = 67043328
 MESH = pl.DeviceIdType.MESH
-
-
-def member_of(position, ranges):
-    return (position >= ranges[0:1, :]) & (position < ranges[8:9, :])
 
 
 def tensor_sums(member, entries):
@@ -29,7 +26,7 @@
     return jnp.sum(jnp.where(member, squares, 0.0), axis=0, keepdims=True)
 
 
-def arrange(
+def kernel(
     n,
     tensors,
     perm_ref,
@@ -38,55 +35,14 @@
     master_ref,
     first_ref,
     second_ref,
-    blocks_out,
-    state_out,
-    owner_out,
-    ranges_out,
-    raw,
-    sems,
-):
-    rows = master_ref.shape[0]
-    span = rows * LANES
-    loads = []
-    for d in range(n):
-        start = pl.multiple_of(perm_ref[d] * span, LANES)
-        source = grads_ref.at[:, pl.ds(start, span)]
-        loads.append(pltpu.make_async_copy(source, raw.at[d], sems.at[d]))
-    for i, ref in enumerate((master_ref, first_ref, second_ref)):
-        loads.append(pltpu.make_async_copy(ref, state_out.at[i], sems.at[n + i]))
-    for load in loads:
-        load.start()
-    lane = lax.broadcasted_iota(jnp.int32, (8, LANES), 1)
-    low = jnp.full((8, LANES), 2**30, jnp.int32)
-    high = low
-    for t in range(tensors):
-        here = lax.rem(lane, LANES // 2) == t
-        low = jnp.where(here, bounds_ref[t], low)
-        high = jnp.where(here, bounds_ref[t + 1], high)
-    ranges_out[0:8, :] = low
-    ranges_out[8:16, :] = high
-    owner_out[...] = perm_ref[lax.axis_index("dp")] * span + LANES * (
-        lax.broadcasted_iota(jnp.int32, (rows, LANES), 0)
-    )
-    for d in range(n):
-        loads[d].wait()
-        wide = raw[d].astype(jnp.float32).reshape(rows, LANES)
-        blocks_out[d] = wide.astype(jnp.bfloat16)
-    for load in loads[n:]:
-        load.wait()
-
-
-def kernel(
-    n,
-    blocks_ref,
-    state,
-    owner,
-    ranges,
     gathered,
     master_out,
     first_out,
     second_out,
     step_out,
+    raw,
+    blocks,
+    state,
     side_recv,
     pair_send,
     pair_recv,
@@ -94,6 +50,7 @@
     far_send,
     far_recv,
     stats,
+    load_sems,
     side_sems,
     pair_sems,
     far_sems,
@@ -104,6 +61,8 @@
     ag_pair_sems,
 ):
     units = n // 4
+    rows = master_ref.shape[0]
+    span = rows * LANES
     section = lax.axis_index("section")
     me = lax.axis_index("dp")
     core = lax.rem(me, 2)
@@ -129,17 +88,46 @@
 
     lax.fori_loop(1, n, greet, 0)
 
+    loads = []
+    for d in range(n):
+        source = grads_ref.at[:, pl.ds(d * span, span)]
+        loads.append(pltpu.make_async_copy(source, raw.at[d], load_sems.at[d]))
+    for i, ref in enumerate((master_ref, first_ref, second_ref)):
+        loads.append(pltpu.make_async_copy(ref, state.at[i], load_sems.at[n + i]))
+    for load in loads:
+        load.start()
+
     sign = jnp.where(2 * rank < units, units - 1, 1)
     order = [lax.rem(rank + sign * (1 + s), units) for s in range(units)]
 
     def block_of(d):
-        return blocks_ref[d].astype(jnp.float32)
-
-    pl.semaphore_wait(barrier, n - 1)
+        return raw[perm_ref[d]].astype(jnp.float32).reshape(rows, LANES)
+
+    half = LANES // 2
+    lane = lax.broadcasted_iota(jnp.int32, (1, LANES), 1)
+    low_half = lane < half
+    low = jnp.full((1, LANES), 2**30, jnp.int32)
+    high = low
+    for t in range(tensors):
+        here = lax.rem(lane, half) == t
+        low = jnp.where(here, bounds_ref[t], low)
+        high = jnp.where(here, bounds_ref[t + 1], high)
+    position = perm_ref[me] * span + LANES * lax.broadcasted_iota(
+        jnp.int32, (rows, LANES), 0
+    )
+    member = (position >= low) & (position < high)
+
+    for load in loads[:n]:
+        load.wait()
     side_copies = []
     for s in range(units):
+        for c in range(2):
+            block = block_of(device_of(order[s], 1 - side, c))
+            blocks[s, c] = block.astype(jnp.bfloat16)
+        if s == 0:
+            pl.semaphore_wait(barrier, n - 1)
         copy = pltpu.make_async_remote_copy(
-            src_ref=blocks_ref.at[pl.ds(device_of(order[s], 1 - side, 0), 2)],
+            src_ref=blocks.at[s],
             dst_ref=side_recv.at[s],
             send_sem=side_sems.at[0, s],
             recv_sem=side_sems.at[1, s],
@@ -149,9 +137,8 @@
         copy.start()
         side_copies.append(copy)
 
-    half = LANES // 2
-    low_half = lax.broadcasted_iota(jnp.int32, (1, LANES), 1) < half
-    member = member_of(owner[...], ranges)
+    for load in loads[n:]:
+        load.wait()
     weight_row = tensor_sums(member, state[0])
 
     pair_copies = []
@@ -342,39 +329,20 @@
         tensors = bounds.shape[0] - 1
         block = (rows, LANES)
         f32 = jnp.float32
+        results = n * shard * 2 + 5 * shard * 4
         hbm_spec = pl.BlockSpec(memory_space=pltpu.HBM)
         vmem_spec = pl.BlockSpec(memory_space=pltpu.VMEM)
         smem_spec = pl.BlockSpec(memory_space=pltpu.SMEM)
-        arranged = pl.pallas_call(
-            functools.partial(arrange, n, tensors),
-            out_shape=[
-                jax.ShapeDtypeStruct((n,) + block, jnp.bfloat16),
-                jax.ShapeDtypeStruct((3,) + block, f32),
-                jax.ShapeDtypeStruct(block, jnp.int32),
-                jax.ShapeDtypeStruct((16, LANES), jnp.int32),
-            ],
+        outs = pl.pallas_call(
+            functools.partial(kernel, n, tensors),
+            out_shape=[jax.ShapeDtypeStruct((n,) + block, jnp.bfloat16)]
+            + [jax.ShapeDtypeStruct(block, f32)] * 4,
             in_specs=[smem_spec] * 2 + [hbm_spec] * 4,
-            out_specs=[vmem_spec] * 4,
+            out_specs=[vmem_spec] * 5,
             scratch_shapes=[
                 pltpu.VMEM((n, 1, shard), jnp.bfloat16),
-                pltpu.SemaphoreType.DMA((n + 3,)),
-            ],
-            compiler_params=pltpu.CompilerParams(vmem_limit_bytes=32 * 1024 * 1024),
-        )(
-            perm,
-            bounds,
-            grads,
-            master.reshape(block),
-            first_moment.reshape(block),
-            second_moment.reshape(block),
-        )
-        outs = pl.pallas_call(
-            functools.partial(kernel, n),
-            out_shape=[jax.ShapeDtypeStruct((n,) + block, jnp.bfloat16)]
-            + [jax.ShapeDtypeStruct(block, f32)] * 4,
-            in_specs=[vmem_spec] * 4,
-            out_specs=[vmem_spec] * 5,
-            scratch_shapes=[
+                pltpu.VMEM((units, 2) + block, jnp.bfloat16),
+                pltpu.VMEM((3,) + block, f32),
                 pltpu.VMEM((units, 2) + block, jnp.bfloat16),
                 pltpu.VMEM((units,) + block, f32),
                 pltpu.VMEM((units,) + block, f32),
@@ -382,6 +350,7 @@
                 pltpu.VMEM((units,) + block, f32),
                 pltpu.VMEM((units,) + block, f32),
                 pltpu.VMEM((n, 8, LANES), f32),
+                pltpu.SemaphoreType.DMA((n + 3,)),
                 pltpu.SemaphoreType.DMA((2, units)),
                 pltpu.SemaphoreType.DMA((2, units)),
                 pltpu.SemaphoreType.DMA((2, units)),
@@ -394,9 +363,16 @@
             compiler_params=pltpu.CompilerParams(
                 collective_id=0,
                 has_side_effects=True,
-                vmem_limit_bytes=32 * 1024 * 1024,
+                vmem_limit_bytes=VMEM_BYTES - results,
             ),
-        )(*arranged)
+        )(
+            perm,
+            bounds,
+            grads,
+            master.reshape(block),
+            first_moment.reshape(block),
+            second_moment.reshape(block),
+        )
         outs = pl.pallas_call(
             functools.partial(place, n),
             out_shape=[jax.ShapeDtypeStruct((n * rows, LANES), jnp.bfloat16)]

time: 56.2 us -> 53.5 us (0.952)
  Pallas kernels: 49.2 us -> 47 us
  local copies, waits for them, and re-layouts: 5.6 us -> 4.84 us
    pallas_call x2 -> x1, Pallas kernels: 47.4 us -> 45.2 us  [per_device(): pl.pallas_call(functools.partial(kernel, n, tensors), out_shape=[jax.Shap...]
    unnamed x12, local copies, waits for them, and re-layouts: 5.6 us -> 4.84 us
where the time goes in v2:
time: 53.5 us; the launch traced here: 52.5 us
  Pallas kernels  47 us (88%)
  local copies, waits for them, and re-layouts  4.84 us (9%)
  between operations  0.67 us (1%)
    pallas_call x1, Pallas kernels, per_device(): pl.pallas_call(functools.partial(kernel, n, tensors), out_shape=[jax.Shap...  45.2 us
    unnamed x12, local copies, waits for them, and re-layouts  4.84 us
    pallas_call x1, Pallas kernels, per_device(): pl.pallas_call(functools.partial(place, n), out_shape=[jax.ShapeDtypeStru...  1.84 us

profile of v2, /device:TPU:9, one launch (start us, length us, event | category | flops | bytes accessed | tf_op | source)
XLA Modules:
  0.0 52.5 jit_solution(18234352978157687316)
XLA Ops:
  0.6 0.0 copy-start.5
  0.6 45.2 %shard_map.101 = (bf16[16,256,128]{2,1,0:T(8,128)(2,1)}, f32[256,128]{1,0:T(8,128)}, f32[256,128]{1,0:T(8,128)}, f32[256,128]{1,0:T(8,128)}, f32[256,128]{1,0:T(8,128)}) custom-call(s32[16]{0:T(128)} %perm_ref.3, s32[17]{0:T(128)} %bounds_ref.1, bf16[1,524288]{1,0:T(2,128)(2,1)} %grads_ref.1, f32[256,128]{1,0:T(8,128)} %bitcast.8, f32[256,128]{1,0:T(8,128)} %bitcast.9, ...), custom_call_target="tpu_custom_call" | custom-call | tf_op jit(solution)/shard_map/pallas_call | solution.py:336
  45.8 0.0 copy-done.5
  45.8 0.0 copy-start
  45.8 1.2 %copy-done = bf16[16,256,128]{2,1,0:T(8,128)(2,1)S(1)} copy-done((bf16[16,256,128]{2,1,0:T(8,128)(2,1)S(1)}, bf16[16,256,128]{2,1,0:T(8,128)(2,1)}, u32[]{:S(2)}) %copy-start) | copy-done | bytes 1048600
  47.1 0.0 copy-start.1
  47.1 0.9 %copy-done.1 = f32[256,128]{1,0:T(8,128)S(1)} copy-done((f32[256,128]{1,0:T(8,128)S(1)}, f32[256,128]{1,0:T(8,128)}, u32[]{:S(2)}) %copy-start.1) | copy-done | bytes 131096
  48.0 0.0 copy-start.2
  48.0 0.9 %copy-done.2 = f32[256,128]{1,0:T(8,128)S(1)} copy-done((f32[256,128]{1,0:T(8,128)S(1)}, f32[256,128]{1,0:T(8,128)}, u32[]{:S(2)}) %copy-start.2) | copy-done | bytes 131096
  48.9 0.0 copy-start.3
  48.9 0.9 %copy-done.3 = f32[256,128]{1,0:T(8,128)S(1)} copy-done((f32[256,128]{1,0:T(8,128)S(1)}, f32[256,128]{1,0:T(8,128)}, u32[]{:S(2)}) %copy-start.3) | copy-done | bytes 131096
  49.8 0.0 copy-start.4
  49.8 0.9 %copy-done.4 = f32[256,128]{1,0:T(8,128)S(1)} copy-done((f32[256,128]{1,0:T(8,128)S(1)}, f32[256,128]{1,0:T(8,128)}, u32[]{:S(2)}) %copy-start.4) | copy-done | bytes 131096
  50.7 1.8 %shard_map.102 = (bf16[4096,128]{1,0:T(8,128)(2,1)}, f32[256,128]{1,0:T(8,128)}, f32[256,128]{1,0:T(8,128)}, f32[256,128]{1,0:T(8,128)}, f32[256,128]{1,0:T(8,128)}) custom-call(s32[16]{0:T(128)S(1)} %copy-done.5, bf16[16,256,128]{2,1,0:T(8,128)(2,1)S(1)} %copy-done, f32[256,128]{1,0:T(8,128)S(1)} %copy-done.1, f32[256,128]{1,0:T(8,128)S(1)} %copy-done.2, ...), custom_call_target="tpu_custom_call" | custom-call | tf_op jit(solution)/shard_map/pallas_call | solution.py:376
Async XLA Ops:
  0.6 45.2 %copy-start.5 = (s32[16]{0:T(128)S(1)}, s32[16]{0:T(128)}, u32[]{:S(2)}) copy-start(s32[16]{0:T(128)} %perm_ref.3) | copy-start | bytes 196
  45.8 1.2 %copy-start = (bf16[16,256,128]{2,1,0:T(8,128)(2,1)S(1)}, bf16[16,256,128]{2,1,0:T(8,128)(2,1)}, u32[]{:S(2)}) copy-start(bf16[16,256,128]{2,1,0:T(8,128)(2,1)} %get-tuple-element.15.gathered) | copy-start | bytes 3145732
  47.1 0.9 %copy-start.1 = (f32[256,128]{1,0:T(8,128)S(1)}, f32[256,128]{1,0:T(8,128)}, u32[]{:S(2)}) copy-start(f32[256,128]{1,0:T(8,128)} %get-tuple-element.16.refs_0_) | copy-start | bytes 393220
  48.0 0.9 %copy-start.2 = (f32[256,128]{1,0:T(8,128)S(1)}, f32[256,128]{1,0:T(8,128)}, u32[]{:S(2)}) copy-start(f32[256,128]{1,0:T(8,128)} %get-tuple-element.17.refs_1_) | copy-start | bytes 393220
  48.9 0.9 %copy-start.3 = (f32[256,128]{1,0:T(8,128)S(1)}, f32[256,128]{1,0:T(8,128)}, u32[]{:S(2)}) copy-start(f32[256,128]{1,0:T(8,128)} %get-tuple-element.18.refs_2_) | copy-start | bytes 393220
  49.8 0.9 %copy-start.4 = (f32[256,128]{1,0:T(8,128)S(1)}, f32[256,128]{1,0:T(8,128)}, u32[]{:S(2)}) copy-start(f32[256,128]{1,0:T(8,128)} %get-tuple-element.19.refs_3_) | copy-start | bytes 393220

commit v3 on v2

--- a/solution.py
+++ b/solution.py
@@ -35,7 +35,7 @@
     master_ref,
     first_ref,
     second_ref,
-    gathered,
+    gathered_out,
     master_out,
     first_out,
     second_out,
@@ -50,7 +50,10 @@
     far_send,
     far_recv,
     stats,
+    result,
+    gathered,
     load_sems,
+    store_sems,
     side_sems,
     pair_sems,
     far_sems,
@@ -103,6 +106,16 @@
     def block_of(d):
         return raw[perm_ref[d]].astype(jnp.float32).reshape(rows, LANES)
 
+    parts = 2
+    depth = rows // parts
+
+    def piece(k):
+        return pl.ds(k * depth, depth)
+
+    def part_of(d, k):
+        part = raw[perm_ref[d], :, pl.ds(k * depth * LANES, depth * LANES)]
+        return part.astype(jnp.float32).reshape(depth, LANES)
+
     half = LANES // 2
     lane = lax.broadcasted_iota(jnp.int32, (1, LANES), 1)
     low_half = lane < half
@@ -126,16 +139,17 @@
             blocks[s, c] = block.astype(jnp.bfloat16)
         if s == 0:
             pl.semaphore_wait(barrier, n - 1)
-        copy = pltpu.make_async_remote_copy(
-            src_ref=blocks.at[s],
-            dst_ref=side_recv.at[s],
-            send_sem=side_sems.at[0, s],
-            recv_sem=side_sems.at[1, s],
-            device_id=at(side_id),
-            device_id_type=MESH,
-        )
-        copy.start()
-        side_copies.append(copy)
+        for k in range(parts):
+            copy = pltpu.make_async_remote_copy(
+                src_ref=blocks.at[s, :, piece(k)],
+                dst_ref=side_recv.at[s, :, piece(k)],
+                send_sem=side_sems.at[0, s, k],
+                recv_sem=side_sems.at[1, s, k],
+                device_id=at(side_id),
+                device_id_type=MESH,
+            )
+            copy.start()
+            side_copies.append(copy)
 
     for load in loads[n:]:
         load.wait()
@@ -143,56 +157,57 @@
 
     pair_copies = []
     far_copies = []
-    own_sum = None
-
-    def finish(s):
-        pair_copies[s].wait_recv()
-        total = keep[s] + pair_recv[s]
-        if s == units - 1:
-            return total
-        far_send[s] = total
-        copy = pltpu.make_async_remote_copy(
-            src_ref=far_send.at[s],
-            dst_ref=far_recv.at[rank],
-            send_sem=far_sems.at[0, s],
-            recv_sem=far_sems.at[1, rank],
-            device_id=at(device_of(order[s], side, core)),
-            device_id_type=MESH,
-        )
-        copy.start()
-        far_copies.append(copy)
-        return None
-
-    for s in range(units):
-        side_copies[s].wait_recv()
+
+    def finish(i):
+        s, k = divmod(i, parts)
+        pair_copies[i].wait_recv()
+        far_send[s, piece(k)] = keep[s, piece(k)] + pair_recv[s, piece(k)]
+        if s < units - 1:
+            copy = pltpu.make_async_remote_copy(
+                src_ref=far_send.at[s, piece(k)],
+                dst_ref=far_recv.at[rank, piece(k)],
+                send_sem=far_sems.at[0, s, k],
+                recv_sem=far_sems.at[1, rank, k],
+                device_id=at(device_of(order[s], side, core)),
+                device_id_type=MESH,
+            )
+            copy.start()
+            far_copies.append(copy)
+
+    for i in range(units * parts):
+        s, k = divmod(i, parts)
+        side_copies[i].wait_recv()
         theirs = device_of(order[s], side, 1 - core)
         mine = device_of(order[s], side, core)
-        pair_send[s] = block_of(theirs) + side_recv[s, 1 - core].astype(jnp.float32)
+        near = side_recv[s, 1 - core, piece(k)].astype(jnp.float32)
+        pair_send[s, piece(k)] = part_of(theirs, k) + near
         copy = pltpu.make_async_remote_copy(
-            src_ref=pair_send.at[s],
-            dst_ref=pair_recv.at[s],
-            send_sem=pair_sems.at[0, s],
-            recv_sem=pair_sems.at[1, s],
+            src_ref=pair_send.at[s, piece(k)],
+            dst_ref=pair_recv.at[s, piece(k)],
+            send_sem=pair_sems.at[0, s, k],
+            recv_sem=pair_sems.at[1, s, k],
             device_id=at(pair_id),
             device_id_type=MESH,
         )
         copy.start()
         pair_copies.append(copy)
-        keep[s] = block_of(mine) + side_recv[s, core].astype(jnp.float32)
-        if s >= 1:
-            finish(s - 1)
-    own_sum = finish(units - 1)
-
-    for j in range(1, units):
-        source = lax.rem(rank + j, units)
-        pltpu.make_async_remote_copy(
-            src_ref=far_send.at[0],
-            dst_ref=far_recv.at[source],
-            send_sem=far_sems.at[0, 0],
-            recv_sem=far_sems.at[1, source],
-            device_id=at(side_id),
-            device_id_type=MESH,
-        ).wait_recv()
+        near = side_recv[s, core, piece(k)].astype(jnp.float32)
+        keep[s, piece(k)] = part_of(mine, k) + near
+        if i >= 1:
+            finish(i - 1)
+    finish(units * parts - 1)
+    own_sum = far_send[units - 1]
+
+    for source in order[:-1]:
+        for k in range(parts):
+            pltpu.make_async_remote_copy(
+                src_ref=far_send.at[0, piece(k)],
+                dst_ref=far_recv.at[source, piece(k)],
+                send_sem=far_sems.at[0, 0, k],
+                recv_sem=far_sems.at[1, source, k],
+                device_id=at(side_id),
+                device_id_type=MESH,
+            ).wait_recv()
         own_sum = own_sum + far_recv[source]
 
     own_grad = own_sum / n
@@ -221,8 +236,21 @@
         return carry
 
     lax.fori_loop(1, n, tell, 0)
-    first_out[...] = new_first
-    second_out[...] = new_second
+    stores = []
+
+    def store(i, value, ref):
+        result[i] = value
+        copy = pltpu.make_async_copy(result.at[i], ref, store_sems.at[n + i])
+        copy.start()
+        stores.append(copy)
+
+    def keep_block(d):
+        copy = pltpu.make_async_copy(gathered.at[d], gathered_out.at[d], store_sems.at[d])
+        copy.start()
+        stores.append(copy)
+
+    store(0, new_first, first_out)
+    store(1, new_second, second_out)
 
     def hear(j, total):
         other = lax.rem(me + j, n)
@@ -251,47 +279,57 @@
         )
 
     waits = []
-    ag_side = gather_copy(me, ag_side_sems, rank, side_id)
-    ag_side.start()
-    waits.append(ag_side)
-    for s in range(units - 1):
-        copy = pltpu.make_async_remote_copy(
-            src_ref=gathered.at[me],
-            dst_ref=gathered.at[me],
-            send_sem=ag_far_sems.at[0, s],
-            recv_sem=ag_far_sems.at[1, rank],
-            device_id=at(device_of(order[s], side, core)),
-            device_id_type=MESH,
-        )
+
+    def send(copy):
         copy.start()
         waits.append(copy)
-    ag_pair = gather_copy(me, ag_pair_sems, 2 * rank + side, pair_id)
-    ag_pair.start()
-    waits.append(ag_pair)
-    master_out[...] = new_master
-    step_out[...] = step_taken
-
-    for s in reversed(range(units - 1)):
-        source = order[s]
+
+    send(gather_copy(me, ag_side_sems, rank, side_id))
+    send(gather_copy(me, ag_pair_sems, 2 * rank + side, pair_id))
+    nearest = list(reversed(order[:-1]))
+    for s, target in enumerate(nearest):
+        send(
+            pltpu.make_async_remote_copy(
+                src_ref=gathered.at[me],
+                dst_ref=gathered.at[me],
+                send_sem=ag_far_sems.at[0, s],
+                recv_sem=ag_far_sems.at[1, rank],
+                device_id=at(device_of(target, side, core)),
+                device_id_type=MESH,
+            )
+        )
+    keep_block(me)
+    store(2, new_master, master_out)
+    store(3, step_taken, step_out)
+
+    def from_far(source):
         block = device_of(source, side, core)
         gather_copy(block, ag_far_sems, source, side_id).wait_recv()
-        copy = gather_copy(block, ag_side_sems, source, side_id)
-        copy.start()
-        waits.append(copy)
-        copy = gather_copy(block, ag_pair_sems, 2 * source + side, pair_id)
-        copy.start()
-        waits.append(copy)
-    for s in reversed(range(units)):
-        source = order[s]
+        send(gather_copy(block, ag_side_sems, source, side_id))
+        send(gather_copy(block, ag_pair_sems, 2 * source + side, pair_id))
+        keep_block(block)
+
+    def from_side(source):
         block = device_of(source, 1 - side, core)
         gather_copy(block, ag_side_sems, source, side_id).wait_recv()
-        copy = gather_copy(block, ag_pair_sems, 2 * source + 1 - side, pair_id)
-        copy.start()
-        waits.append(copy)
-    for s in reversed(range(units)):
+        send(gather_copy(block, ag_pair_sems, 2 * source + 1 - side, pair_id))
+        keep_block(block)
+
+    def from_pair(source):
         for y in range(2):
-            block = device_of(order[s], y, 1 - core)
-            gather_copy(block, ag_pair_sems, 2 * order[s] + y, pair_id).wait_recv()
+            block = device_of(source, y, 1 - core)
+            gather_copy(block, ag_pair_sems, 2 * source + y, pair_id).wait_recv()
+            keep_block(block)
+
+    sources = [rank] + nearest
+    for s in range(1, units):
+        from_far(sources[s])
+        from_side(sources[s - 1])
+        if s >= 2:
+            from_pair(sources[s - 2])
+    from_side(sources[-1])
+    for source in sources[max(units - 2, 0):]:
+        from_pair(source)
 
     for copy in side_copies + pair_copies + far_copies + waits:
         copy.wait_send()
@@ -302,21 +340,30 @@
         return carry
 
     lax.fori_loop(1, n, told, 0)
+    for copy in stores:
+        copy.wait()
 
 def place(n, perm_ref, gathered, *refs):
-    held, (weights_out, *outs, sems) = refs[:4], refs[4:]
+    held, (weights_out, *outs), (blocks, arrays, sems) = refs[:4], refs[4:9], refs[9:]
     rows = gathered.shape[1]
-    copies = []
+    loads, stores = [], []
     for d in range(n):
         start = pl.multiple_of(perm_ref[d] * rows, rows)
         target = weights_out.at[pl.ds(start, rows)]
-        copies.append(pltpu.make_async_copy(gathered.at[d], target, sems.at[d]))
+        loads.append(pltpu.make_async_copy(gathered.at[d], blocks.at[d], sems.at[0, d]))
+        stores.append(pltpu.make_async_copy(blocks.at[d], target, sems.at[1, d]))
     for i, (ref, out) in enumerate(zip(held, outs)):
-        copies.append(pltpu.make_async_copy(ref, out, sems.at[n + i]))
-    for copy in copies:
-        copy.start()
-    for copy in copies:
-        copy.wait()
+        sem = sems.at[0, n + i]
+        loads.append(pltpu.make_async_copy(ref, arrays.at[i], sem))
+        sem = sems.at[1, n + i]
+        stores.append(pltpu.make_async_copy(arrays.at[i], out, sem))
+    for load in loads:
+        load.start()
+    for load, store in zip(loads, stores):
+        load.wait()
+        store.start()
+    for store in stores:
+        store.wait()
 
 
 def solution(mesh):
@@ -329,16 +376,14 @@
         tensors = bounds.shape[0] - 1
         block = (rows, LANES)
         f32 = jnp.float32
-        results = n * shard * 2 + 5 * shard * 4
         hbm_spec = pl.BlockSpec(memory_space=pltpu.HBM)
-        vmem_spec = pl.BlockSpec(memory_space=pltpu.VMEM)
         smem_spec = pl.BlockSpec(memory_space=pltpu.SMEM)
         outs = pl.pallas_call(
             functools.partial(kernel, n, tensors),
             out_shape=[jax.ShapeDtypeStruct((n,) + block, jnp.bfloat16)]
             + [jax.ShapeDtypeStruct(block, f32)] * 4,
             in_specs=[smem_spec] * 2 + [hbm_spec] * 4,
-            out_specs=[vmem_spec] * 5,
+            out_specs=[hbm_spec] * 5,
             scratch_shapes=[
                 pltpu.VMEM((n, 1, shard), jnp.bfloat16),
                 pltpu.VMEM((units, 2) + block, jnp.bfloat16),
@@ -350,10 +395,13 @@
                 pltpu.VMEM((units,) + block, f32),
                 pltpu.VMEM((units,) + block, f32),
                 pltpu.VMEM((n, 8, LANES), f32),
+                pltpu.VMEM((4,) + block, f32),
+                pltpu.VMEM((n,) + block, jnp.bfloat16),
                 pltpu.SemaphoreType.DMA((n + 3,)),
-                pltpu.SemaphoreType.DMA((2, units)),
-                pltpu.SemaphoreType.DMA((2, units)),
-                pltpu.SemaphoreType.DMA((2, units)),
+                pltpu.SemaphoreType.DMA((n + 4,)),
+                pltpu.SemaphoreType.DMA((2, units, 2)),
+                pltpu.SemaphoreType.DMA((2, units, 2)),
+                pltpu.SemaphoreType.DMA((2, units, 2)),
                 pltpu.SemaphoreType.DMA((n,)),
                 pltpu.SemaphoreType.DMA((n,)),
                 pltpu.SemaphoreType.DMA((2, units)),
@@ -363,7 +411,7 @@
             compiler_params=pltpu.CompilerParams(
                 collective_id=0,
                 has_side_effects=True,
-                vmem_limit_bytes=VMEM_BYTES - results,
+                vmem_limit_bytes=VMEM_BYTES,
             ),
         )(
             perm,
@@ -377,10 +425,14 @@
             functools.partial(place, n),
             out_shape=[jax.ShapeDtypeStruct((n * rows, LANES), jnp.bfloat16)]
             + [jax.ShapeDtypeStruct(block, f32)] * 4,
-            in_specs=[smem_spec] + [vmem_spec] * 5,
+            in_specs=[smem_spec] + [hbm_spec] * 5,
             out_specs=[hbm_spec] * 5,
-            scratch_shapes=[pltpu.SemaphoreType.DMA((n + 4,))],
-            compiler_params=pltpu.CompilerParams(vmem_limit_bytes=32 * 1024 * 1024),
+            scratch_shapes=[
+                pltpu.VMEM((n,) + block, jnp.bfloat16),
+                pltpu.VMEM((4,) + block, f32),
+                pltpu.SemaphoreType.DMA((2, n + 4)),
+            ],
+            compiler_params=pltpu.CompilerParams(vmem_limit_bytes=VMEM_BYTES),
         )(perm, *outs)
         weights = outs[0].reshape(-1)
         return (weights,) + tuple(out.reshape(1, shard) for out in outs[1:])

time: 53.5 us -> 47.6 us (0.89); the launches traced: 52.5 us -> 47.4 us
  local copies, waits for them, and re-layouts: 4.84 us -> 0 us
    unnamed x12 -> x0, local copies, waits for them, and re-layouts: 4.84 us -> none
    pallas_call x1, Pallas kernels: 45.2 us -> 43.6 us  [per_device(): pl.pallas_call(functools.partial(kernel, n, tensors), out_shape=[jax.Shap...]
    pallas_call x1, Pallas kernels: 1.84 us -> 3.14 us  [per_device(): pl.pallas_call(functools.partial(place, n), out_shape=[jax.ShapeDtypeStru...]
where the time goes in v3:
time: 47.6 us; the launch traced here: 47.4 us
  Pallas kernels  46.8 us (98%)
  between operations  0.64 us (1%)
    pallas_call x1, Pallas kernels, per_device(): pl.pallas_call(functools.partial(kernel, n, tensors), out_shape=[jax.Shap...  43.6 us
    pallas_call x1, Pallas kernels, per_device(): pl.pallas_call(functools.partial(place, n), out_shape=[jax.ShapeDtypeStru...  3.14 us

profile of v3, /device:TPU:9, one launch (start us, length us, event | category | flops | bytes accessed | tf_op | source)
XLA Modules:
  0.0 47.4 jit_solution(6899732255846922866)
XLA Ops:
  0.6 43.6 %shard_map.101 = (bf16[16,256,128]{2,1,0:T(8,128)(2,1)}, f32[256,128]{1,0:T(8,128)}, f32[256,128]{1,0:T(8,128)}, f32[256,128]{1,0:T(8,128)}, f32[256,128]{1,0:T(8,128)}) custom-call(s32[16]{0:T(128)} %perm_ref.3, s32[17]{0:T(128)} %bounds_ref.1, bf16[1,524288]{1,0:T(2,128)(2,1)} %grads_ref.1, f32[256,128]{1,0:T(8,128)} %bitcast.8, f32[256,128]{1,0:T(8,128)} %bitcast.9, ...), custom_call_target="tpu_custom_call" | custom-call | tf_op jit(solution)/shard_map/pallas_call | solution.py:381
  44.2 3.1 %shard_map.102 = (bf16[4096,128]{1,0:T(8,128)(2,1)}, f32[256,128]{1,0:T(8,128)}, f32[256,128]{1,0:T(8,128)}, f32[256,128]{1,0:T(8,128)}, f32[256,128]{1,0:T(8,128)}) custom-call(s32[16]{0:T(128)} %perm_ref.3, bf16[16,256,128]{2,1,0:T(8,128)(2,1)} %get-tuple-element.15.gathered, f32[256,128]{1,0:T(8,128)} %get-tuple-element.16.refs_0_, ...), custom_call_target="tpu_custom_call" | custom-call | tf_op jit(solution)/shard_map/pallas_call | solution.py:424

commit v4 on v3

--- a/solution.py
+++ b/solution.py
@@ -18,6 +18,7 @@
 
 LANES = 128
 VMEM_BYTES = 67043328
+PARTS = 4
 MESH = pl.DeviceIdType.MESH
 
 
@@ -62,6 +63,8 @@
     ag_far_sems,
     ag_side_sems,
     ag_pair_sems,
+    right_sem,
+    left_sem,
 ):
     units = n // 4
     rows = master_ref.shape[0]
@@ -83,13 +86,52 @@
 
     barrier = pltpu.get_barrier_semaphore()
 
-    def greet(j, carry):
-        pl.semaphore_signal(
-            barrier, inc=1, device_id=at(lax.rem(me + j, n)), device_id_type=MESH
-        )
-        return carry
-
-    lax.fori_loop(1, n, greet, 0)
+    def signal(sem, index):
+        pl.semaphore_signal(sem, inc=1, device_id=at(index), device_id_type=MESH)
+
+    column = [device_of(rank - 1, side, core), device_of(rank + 1, side, core)]
+    has_left, has_right = rank > 0, rank < units - 1
+    signal(barrier, pair_id)
+    signal(barrier, side_id)
+    signal(barrier, device_of(rank, 1 - side, 1 - core))
+
+    @pl.when(has_left)
+    def _():
+        signal(barrier, column[0])
+
+    @pl.when(has_right)
+    def _():
+        signal(barrier, column[1])
+
+    def enter():
+        sides = jnp.where(has_left & has_right, 2, 1)
+        pl.semaphore_wait(barrier, 3 + sides)
+
+    def relay(sem, has_before, has_after, after):
+        @pl.when(has_before)
+        def _():
+            pl.semaphore_wait(sem, 1)
+
+        @pl.when(has_after)
+        def _():
+            signal(sem, after)
+
+    def enter_all():
+        def rightward():
+            relay(right_sem, has_left, has_right, column[1])
+
+        def leftward():
+            relay(left_sem, has_right, has_left, column[0])
+
+        @pl.when(2 * rank < units)
+        def _():
+            rightward()
+            leftward()
+
+        @pl.when(2 * rank >= units)
+        def _():
+            leftward()
+            rightward()
 
     loads = []
     for d in range(n):
@@ -106,7 +148,7 @@
     def block_of(d):
         return raw[perm_ref[d]].astype(jnp.float32).reshape(rows, LANES)
 
-    parts = 2
+    parts = PARTS
     depth = rows // parts
 
     def piece(k):
@@ -138,7 +180,7 @@
             block = block_of(device_of(order[s], 1 - side, c))
             blocks[s, c] = block.astype(jnp.bfloat16)
         if s == 0:
-            pl.semaphore_wait(barrier, n - 1)
+            enter()
         for k in range(parts):
             copy = pltpu.make_async_remote_copy(
                 src_ref=blocks.at[s, :, piece(k)],
@@ -153,6 +195,7 @@
 
     for load in loads[n:]:
         load.wait()
+    enter_all()
     weight_row = tensor_sums(member, state[0])
 
     pair_copies = []
@@ -231,11 +274,14 @@
             device_id_type=MESH,
         )
 
-    def tell(j, carry):
-        stat_copy(me, lax.rem(me + j, n)).start()
-        return carry
-
-    lax.fori_loop(1, n, tell, 0)
+    others = [
+        device_of(r, y, c)
+        for r in order
+        for y in (1 - side, side)
+        for c in (1 - core, core)
+    ][:-1]
+    for other in others:
+        stat_copy(me, other).start()
     stores = []
 
     def store(i, value, ref):
@@ -252,12 +298,10 @@
     store(0, new_first, first_out)
     store(1, new_second, second_out)
 
-    def hear(j, total):
-        other = lax.rem(me + j, n)
+    total = stat
+    for other in reversed(others):
         stat_copy(other, other).wait_recv()
-        return total + stats[other, pl.ds(0, 1)]
-
-    total = lax.fori_loop(1, n, hear, stat)
+        total = total + stats[other, pl.ds(0, 1)]
     trust_ratio = jnp.sqrt(total) / (
         jnp.sqrt(pltpu.roll(total, half, 1)) + norm_eps
     )
@@ -286,8 +330,8 @@
 
     send(gather_copy(me, ag_side_sems, rank, side_id))
     send(gather_copy(me, ag_pair_sems, 2 * rank + side, pair_id))
-    nearest = list(reversed(order[:-1]))
-    for s, target in enumerate(nearest):
+    ranked = order[:-1]
+    for s, target in enumerate(ranked):
         send(
             pltpu.make_async_remote_copy(
                 src_ref=gathered.at[me],
@@ -321,7 +365,7 @@
             gather_copy(block, ag_pair_sems, 2 * source + y, pair_id).wait_recv()
             keep_block(block)
 
-    sources = [rank] + nearest
+    sources = [rank] + ranked
     for s in range(1, units):
         from_far(sources[s])
         from_side(sources[s - 1])
@@ -334,12 +378,8 @@
     for copy in side_copies + pair_copies + far_copies + waits:
         copy.wait_send()
 
-    def told(j, carry):
-        target = lax.rem(me + j, n)
-        stat_copy(me, target).wait_send()
-        return carry
-
-    lax.fori_loop(1, n, told, 0)
+    for other in others:
+        stat_copy(me, other).wait_send()
     for copy in stores:
         copy.wait()
 
@@ -399,14 +439,16 @@
                 pltpu.VMEM((n,) + block, jnp.bfloat16),
                 pltpu.SemaphoreType.DMA((n + 3,)),
                 pltpu.SemaphoreType.DMA((n + 4,)),
-                pltpu.SemaphoreType.DMA((2, units, 2)),
-                pltpu.SemaphoreType.DMA((2, units, 2)),
-                pltpu.SemaphoreType.DMA((2, units, 2)),
+                pltpu.SemaphoreType.DMA((2, units, PARTS)),
+                pltpu.SemaphoreType.DMA((2, units, PARTS)),
+                pltpu.SemaphoreType.DMA((2, units, PARTS)),
                 pltpu.SemaphoreType.DMA((n,)),
                 pltpu.SemaphoreType.DMA((n,)),
                 pltpu.SemaphoreType.DMA((2, units)),
                 pltpu.SemaphoreType.DMA((2, units)),
                 pltpu.SemaphoreType.DMA((2, 2 * units)),
+                pltpu.SemaphoreType.REGULAR,
+                pltpu.SemaphoreType.REGULAR,
             ],
             compiler_params=pltpu.CompilerParams(
                 collective_id=0,

time: 47.6 us -> 46.2 us (0.971)
  Pallas kernels: 46.8 us -> 45.1 us
    pallas_call x1, Pallas kernels: 43.6 us -> 42 us  [per_device(): pl.pallas_call(functools.partial(kernel, n, tensors), out_shape=[jax.Shap...]
where the time goes in v4:
time: 46.2 us; the launch traced here: 45.8 us
  Pallas kernels  45.1 us (98%)
  between operations  0.64 us (1%)
    pallas_call x1, Pallas kernels, per_device(): pl.pallas_call(functools.partial(kernel, n, tensors), out_shape=[jax.Shap...  42 us
    pallas_call x1, Pallas kernels, per_device(): pl.pallas_call(functools.partial(place, n), out_shape=[jax.ShapeDtypeStru...  3.14 us

profile of v4, /device:TPU:9, one launch (start us, length us, event | category | flops | bytes accessed | tf_op | source)
XLA Modules:
  0.0 45.8 jit_solution(5404480117273595726)
XLA Ops:
  0.6 42.0 %shard_map.101 = (bf16[16,256,128]{2,1,0:T(8,128)(2,1)}, f32[256,128]{1,0:T(8,128)}, f32[256,128]{1,0:T(8,128)}, f32[256,128]{1,0:T(8,128)}, f32[256,128]{1,0:T(8,128)}) custom-call(s32[16]{0:T(128)} %perm_ref.3, s32[17]{0:T(128)} %bounds_ref.1, bf16[1,524288]{1,0:T(2,128)(2,1)} %grads_ref.1, f32[256,128]{1,0:T(8,128)} %bitcast.8, f32[256,128]{1,0:T(8,128)} %bitcast.9, ...), custom_call_target="tpu_custom_call" | custom-call | tf_op jit(solution)/shard_map/pallas_call | solution.py:421
  42.6 3.1 %shard_map.102 = (bf16[4096,128]{1,0:T(8,128)(2,1)}, f32[256,128]{1,0:T(8,128)}, f32[256,128]{1,0:T(8,128)}, f32[256,128]{1,0:T(8,128)}, f32[256,128]{1,0:T(8,128)}) custom-call(s32[16]{0:T(128)} %perm_ref.3, bf16[16,256,128]{2,1,0:T(8,128)(2,1)} %get-tuple-element.15.gathered, f32[256,128]{1,0:T(8,128)} %get-tuple-element.16.refs_0_, ...), custom_call_target="tpu_custom_call" | custom-call | tf_op jit(solution)/shard_map/pallas_call | solution.py:466
